TPU v7x, 512 devices: a 8x2x16 block of a 8x8x16 slice. The times are simulated.
512 devices in a mesh: group: 2 (over y), plane: 16 (over z), planey: 8 (over x), ens: 2 (over core).
Axes of the slice: x: 8, y: 2, z: 16, core: 2. Of those that a mesh axis runs over, the one named last changes fastest.
The devices are a block of a 8x8x16 slice.
Arguments:
- u_prior: float32 [8, 2, 10, 256, 1024], P(('group', 'ens'), None, None, 'plane', 'planey'), parts along dimension 0, may hold values from -6 to 6
- friction_rows: int32 [8], P(('group', 'ens')), parts along dimension 0, may hold values from 0 to 15
- friction_table: float32 [32, 256, 1024], P('group', 'plane', 'planey'), parts along dimension 0, may hold values from 0.3 to 3
- bed_fixed: int32 [256, 1024], P('plane', 'planey'), may hold values from -536870912 to 536870911
- ice_mask: int32 [256, 1024], P('plane', 'planey'), may hold values 0 or 1
Outputs:
- mean_velocity: float32 [4, 10, 256, 1024], P('group', None, 'plane', 'planey'), parts along dimension 0
There are 2 independent parts, one for each index of `group`. A program takes and returns all parts, laid end to end along the dimension named above; an argument that names none is the same for every part. Nothing has to cross between parts.
Inputs may be any that keep to these rules, and one draw needn't show every extreme that they name: `friction_rows`: each sample names one row of the friction table.
All inputs are finite; a program needn't handle non-finite values. No bound on the sum of `ice_mask` on one device may be relied on, other than what follows from the above.
Results may differ from a plain program's by a relative error of at most 0.0003.
Values sent between devices are 32-bit elements; how exact they have to be, the bound alone decides.
No kernel may reach another device: no remote copies, remote signals or barrier semaphores. Data moves between devices by JAX's collectives and lax.ppermute only.
A program may use at most 64 MiB of HBM per device.

v0:
```python
import jax
import jax.numpy as jnp
from jax import lax
from jax.sharding import PartitionSpec as P

bed_unit = 2.0 ** (-29)
factor_u = (2.0, 1.0, 0.5)
factor_v = (2.0, 0.5, 1.0)


def extended_2(cells, sides, width):
    for axis, dim in sides:
        count = lax.axis_size(axis)
        ends = count - 1
        head = lax.slice_in_dim(cells, 0, width, axis=dim)
        tail = lax.slice_in_dim(cells, cells.shape[dim] - width, cells.shape[dim], axis=dim)
        cells = jnp.concatenate(
            [
                lax.ppermute(tail, axis, [(i, (i + 1) % count) for i in range(ends)]),
                cells,
                lax.ppermute(head, axis, [((i + 1) % count, i) for i in range(ends)]),
            ],
            axis=dim,
        )
    return cells


def one_axis_at_a_time(value, axes):
    for axis in axes:
        value = lax.psum(value, axis)
    return value


def total_of_pieces(value, axis):
    blocks = lax.all_gather(value, axis)
    return blocks.sum(axis=0)


def coefficient(offset):
    nonzero = len([entry for entry in offset if entry != 0])
    weight_u = 0.25 ** (nonzero - 1)
    weight_v = weight_u
    for dimension in range(3):
        if offset[dimension] != 0:
            weight_u = weight_u * factor_u[dimension]
            weight_v = weight_v * factor_v[dimension]
    return jnp.array([weight_u, weight_v], jnp.float32).reshape(2, 1, 1, 1)


def neighbour_sum(padded):
    layers = padded.shape[-3] - 2
    span_x = padded.shape[-2] - 2
    span_y = padded.shape[-1] - 2
    summed = None
    for step_z in (-1, 0, 1):
        for step_x in (-1, 0, 1):
            for step_y in (-1, 0, 1):
                if step_z == 0 and step_x == 0 and (step_y == 0):
                    continue
                window = padded[
                    ...,
                    1 + step_z : 1 + step_z + layers,
                    1 + step_x : 1 + step_x + span_x,
                    1 + step_y : 1 + step_y + span_y,
                ]
                addend = coefficient((step_z, step_x, step_y)) * window
                summed = addend if summed is None else summed + addend
    return summed


def strain_roots(extended):
    padded = jnp.pad(extended, [(0, 0)] * (extended.ndim - 3) + [(1, 1), (0, 0), (0, 0)])
    along_x = (padded[..., 1:-1, 2:, 1:-1] - padded[..., 1:-1, :-2, 1:-1]) * 0.5
    along_y = (padded[..., 1:-1, 1:-1, 2:] - padded[..., 1:-1, 1:-1, :-2]) * 0.5
    along_z = (padded[..., 2:, 1:-1, 1:-1] - padded[..., :-2, 1:-1, 1:-1]) * 0.5
    stretch_x = along_x[..., 0, :, :, :]
    stretch_y = along_y[..., 1, :, :, :]
    shear_one = along_y[..., 0, :, :, :]
    shear_two = along_x[..., 1, :, :, :]
    vertical_u = along_z[..., 0, :, :, :]
    vertical_v = along_z[..., 1, :, :, :]
    shear = shear_one + shear_two
    strain = (
        stretch_x * stretch_x
        + stretch_y * stretch_y
        + stretch_x * stretch_y
        + 0.25 * shear * shear
        + 0.25 * (vertical_u * vertical_u + vertical_v * vertical_v)
    )
    return jnp.power(strain + 0.1, -1.0 / 6.0)[..., None, :, :, :]


def pad_layers(field):
    return jnp.pad(field, ((0, 0), (0, 0), (1, 1), (0, 0), (0, 0)))


def inner(left, right):
    return jnp.sum(left * right, axis=(1, 2, 3, 4))


def spread(values):
    return values.reshape(-1, 1, 1, 1, 1)


def trimmed(field, margin):
    return field[..., margin:-margin, margin:-margin]


def apply_local(roots_wide, across_part, diag_part, field_wide):
    product = roots_wide * field_wide
    nearby = neighbour_sum(pad_layers(product))
    centre = trimmed(field_wide, 1)
    return trimmed(roots_wide, 1) * (across_part * centre - nearby) + diag_part * centre


def body(u_prior, friction_rows, friction_table, bed_fixed, ice_mask):
    members = u_prior.shape[0]
    layers = u_prior.shape[2]
    rows_x = u_prior.shape[3]
    rows_y = u_prior.shape[4]
    total_x = rows_x * lax.axis_size("plane")
    cover = ice_mask.astype(jnp.float32)
    bed_block = (bed_fixed.astype(jnp.float32) * bed_unit).reshape(1, 1, 1, rows_x, rows_y)
    levels = jnp.arange(friction_table.shape[0], dtype=jnp.int32)
    chosen = (friction_rows[:, None] == levels[None, :]).astype(jnp.float32)
    friction = jnp.sum(chosen[:, :, None, None] * friction_table[None], axis=1)
    bottom = (
        (jnp.arange(layers, dtype=jnp.int32) == 0).astype(jnp.float32).reshape(1, 1, layers, 1, 1)
    )
    mask_block = cover.reshape(1, 1, 1, rows_x, rows_y)
    friction_block = friction.reshape(members, 1, 1, rows_x, rows_y)
    prior_wide, bed_wide, mask_wide, friction_wide = (
        extended_2(u_prior, (("plane", 3), ("planey", 4)), 4),
        extended_2(bed_block, (("plane", 3), ("planey", 4)), 4),
        extended_2(mask_block, (("plane", 3), ("planey", 4)), 4),
        extended_2(friction_block, (("plane", 3), ("planey", 4)), 4),
    )
    roots_three = trimmed(mask_wide, 1) * strain_roots(prior_wide)
    across_two = neighbour_sum(pad_layers(roots_three))
    bed_three = trimmed(bed_wide, 1)
    slope_x = (bed_three[..., 2:, 1:-1] - bed_three[..., :-2, 1:-1]) * 0.5
    slope_y = (bed_three[..., 1:-1, 2:] - bed_three[..., 1:-1, :-2]) * 0.5
    mask_two = trimmed(mask_wide, 2)
    position = (
        lax.axis_index("plane") * rows_x - 2 + jnp.arange(rows_x + 4, dtype=jnp.int32)
    ).astype(jnp.float32)
    thickness = 1.0 + 2.0 * position[:, None] / (total_x - 1)
    force_two = jnp.concatenate(
        [-(mask_two * thickness * slope_x), -(mask_two * thickness * slope_y)], axis=1
    )
    diag_two = mask_two * trimmed(friction_wide, 2) * bottom + (1.0 - mask_two)
    start_three = trimmed(prior_wide, 1) * trimmed(mask_wide, 1)
    residual_two = force_two - apply_local(roots_three, across_two, diag_two, start_three)
    image_one = apply_local(
        trimmed(roots_three, 1), trimmed(across_two, 1), trimmed(diag_two, 1), residual_two
    )
    second_image = apply_local(
        trimmed(roots_three, 2), trimmed(across_two, 2), trimmed(diag_two, 2), image_one
    )
    residual = trimmed(residual_two, 2)
    image = trimmed(image_one, 1)
    gram_rr, gram_ra, gram_aa, gram_ab = (
        one_axis_at_a_time(inner(residual, residual), ("plane", "planey")),
        one_axis_at_a_time(inner(residual, image), ("plane", "planey")),
        one_axis_at_a_time(inner(image, image), ("plane", "planey")),
        one_axis_at_a_time(inner(image, second_image), ("plane", "planey")),
    )
    first_step = gram_rr / gram_ra
    norm_next = gram_rr - 2.0 * first_step * gram_ra + first_step * first_step * gram_aa
    growth = 1.0 + norm_next / gram_rr
    curve = (
        growth * growth * gram_ra
        - 2.0 * growth * first_step * gram_aa
        + first_step * first_step * gram_ab
    )
    second_step = norm_next / curve
    solution = trimmed(start_three, 3)
    solution = (
        solution
        + spread(first_step + second_step * growth) * residual
        - spread(second_step * first_step) * image
    )
    local_sum = jnp.sum(solution, axis=0)
    summed = total_of_pieces(local_sum, "ens")
    return summed / (members * lax.axis_size("ens"))


def solution(mesh):
    in_specs = (
        P(("group", "ens"), None, None, "plane", "planey"),
        P(("group", "ens")),
        P("group", "plane", "planey"),
        P("plane", "planey"),
        P("plane", "planey"),
    )
    out_specs = P("group", None, "plane", "planey")
    return jax.shard_map(body, mesh=mesh, in_specs=in_specs, out_specs=out_specs, check_vma=False)
```

profile of v0, /device:TPU:65, one launch (start us, length us, event | category | flops | bytes accessed | tf_op | source)
XLA Modules:
  0.0 188.2 jit_solution(14085209569929018749)
XLA Ops:
  0.0 0.7 convert_bitcast_fusion
  0.7 6.6 %collective-permute-start.4 = (f32[1,1,1,4,128]{4,3,2,1,0:T(4,128)S(1)}, f32[1,1,1,4,128]{4,3,2,1,0:T(4,128)S(1)}, u32[]{:S(2)}, u32[]{:S(2)}) collective-permute-start(f32[1,1,1,4,128]{4,3,2,1,0:T(4,128)S(1)} %get-tuple-element.76), channel_id=1, source_target_pairs={{0,16},{16,32},{32,48},{48,64},{64,80},{80,96},{96,112},{112,128},... | collective-permute-start | bytes 6152 | tf_op jit(solution)/shard_map/ppermute | solution.py:19
  7.3 1.3 collective-permute-start.5
  8.6 0.7 multiply_bitcast_fusion
  9.3 6.4 %collective-permute-start.8 = (f32[1,1,1,4,128]{4,3,2,1,0:T(4,128)S(1)}, f32[1,1,1,4,128]{4,3,2,1,0:T(4,128)S(1)}, u32[]{:S(2)}, u32[]{:S(2)}) collective-permute-start(f32[1,1,1,4,128]{4,3,2,1,0:T(4,128)S(1)} %get-tuple-element.74), channel_id=1, source_target_pairs={{0,16},{16,32},{32,48},{48,64},{64,80},{80,96},{96,112},{112,128},... | collective-permute-start | bytes 6152 | tf_op jit(solution)/shard_map/ppermute | solution.py:19
  15.7 1.3 collective-permute-start.9
  17.0 0.7 compare_convert_fusion.1
  17.7 1.0 multiply_reduce_fusion.3
  18.7 6.4 %collective-permute-start.12 = (f32[2,1,1,4,128]{4,3,0,2,1:T(4,128)S(1)}, f32[2,1,1,4,128]{4,3,0,2,1:T(4,128)S(1)}, u32[]{:S(2)}, u32[]{:S(2)}) collective-permute-start(f32[2,1,1,4,128]{4,3,0,2,1:T(4,128)S(1)} %get-tuple-element.68), channel_id=1, source_target_pairs={{0,16},{16,32},{32,48},{48,64},{64,80},{80,96},{96,112},{112,128},... | collective-permute-start | bytes 12296 | tf_op jit(solution)/shard_map/ppermute | solution.py:19
  25.2 1.0 fusion.197
  26.2 1.3 collective-permute-start.13
  27.5 7.6 %collective-permute-start = (f32[2,2,10,4,128]{4,3,2,1,0:T(4,128)S(1)}, f32[2,2,10,4,128]{4,3,2,1,0:T(4,128)S(1)}, u32[]{:S(2)}, u32[]{:S(2)}) collective-permute-start(f32[2,2,10,4,128]{4,3,2,1,0:T(4,128)S(1)} %get-tuple-element.60), channel_id=1, source_target_pairs={{0,16},{16,32},{32,48},{48,64},{64,80},{80,96},{96,112},{112,128},... | collective-permute-start | bytes 245768 | tf_op jit(solution)/shard_map/ppermute | solution.py:19
  35.3 3.3 %collective-permute-start.6 = (f32[1,1,1,24,4]{4,3,2,1,0:T(8,128)S(1)}, f32[1,1,1,24,4]{4,3,2,1,0:T(8,128)S(1)}, u32[]{:S(2)}, u32[]{:S(2)}) collective-permute-start(f32[1,1,1,24,4]{4,3,2,1,0:T(8,128)S(1)} %get-tuple-element.72), channel_id=1, source_target_pairs={{0,2},{2,4},{4,6},{6,8},{8,10},{10,12},{12,14},{1,3},{3,5},{5,7},{... | collective-permute-start | bytes 1160 | tf_op jit(solution)/shard_map/ppermute | solution.py:19
  38.5 1.3 collective-permute-start.7
  40.0 4.0 %collective-permute-start.10 = (f32[1,1,1,24,4]{4,3,2,1,0:T(8,128)S(1)}, f32[1,1,1,24,4]{4,3,2,1,0:T(8,128)S(1)}, u32[]{:S(2)}, u32[]{:S(2)}) collective-permute-start(f32[1,1,1,24,4]{4,3,2,1,0:T(8,128)S(1)} %get-tuple-element.70), channel_id=1, source_target_pairs={{0,2},{2,4},{4,6},{6,8},{8,10},{10,12},{12,14},{1,3},{3,5},{5,7},{... | collective-permute-start | bytes 1160 | tf_op jit(solution)/shard_map/ppermute | solution.py:19
  44.0 1.3 collective-permute-start.11
  45.4 1.3 collective-permute-start.1
  46.7 1.8 collective-permute-done.11
  48.6 0.1 fusion.193
  48.9 4.2 %collective-permute-start.14 = (f32[2,1,1,24,4]{4,3,0,2,1:T(8,128)S(1)}, f32[2,1,1,24,4]{4,3,0,2,1:T(8,128)S(1)}, u32[]{:S(2)}, u32[]{:S(2)}) collective-permute-start(f32[2,1,1,24,4]{4,3,0,2,1:T(8,128)S(1)} %get-tuple-element.66), channel_id=1, source_target_pairs={{0,2},{2,4},{4,6},{6,8},{8,10},{10,12},{12,14},{1,3},{3,5},{5,7},{... | collective-permute-start | bytes 2312 | tf_op jit(solution)/shard_map/ppermute | solution.py:19
  53.1 1.3 collective-permute-start.15
  54.5 4.5 %collective-permute-done.15 = f32[2,1,1,24,4]{4,3,0,2,1:T(8,128)S(1)} collective-permute-done((f32[2,1,1,24,4]{4,3,0,2,1:T(8,128)S(1)}, f32[2,1,1,24,4]{4,3,0,2,1:T(8,128)S(1)}, u32[]{:S(2)}, u32[]{:S(2)}) %collective-permute-start.15) | collective-permute-done | bytes 800 | tf_op jit(solution)/shard_map/ppermute | solution.py:21
  59.1 0.1 multiply_add_fusion
  59.2 0.2 slice_bitcast_fusion
  59.5 0.5 copy-done
  60.1 0.2 fusion.196
  60.3 4.6 %collective-permute-start.2 = (f32[2,2,10,24,4]{4,3,2,1,0:T(8,128)S(1)}, f32[2,2,10,24,4]{4,3,2,1,0:T(8,128)S(1)}, u32[]{:S(2)}, u32[]{:S(2)}) collective-permute-start(f32[2,2,10,24,4]{4,3,2,1,0:T(8,128)S(1)} %get-tuple-element.58), channel_id=1, source_target_pairs={{0,2},{2,4},{4,6},{6,8},{8,10},{10,12},{12,14},{1,3},{3,5},{5,7},{... | collective-permute-start | bytes 46088 | tf_op jit(solution)/shard_map/ppermute | solution.py:19
  64.9 1.5 collective-permute-start.3
  66.4 0.1 slice_bitcast_fusion.7
  66.5 4.2 %collective-permute-done.2 = f32[2,2,10,24,4]{4,3,2,1,0:T(8,128)S(1)} collective-permute-done((f32[2,2,10,24,4]{4,3,2,1,0:T(8,128)S(1)}, f32[2,2,10,24,4]{4,3,2,1,0:T(8,128)S(1)}, u32[]{:S(2)}, u32[]{:S(2)}) %collective-permute-start.2) | collective-permute-done | bytes 15392 | tf_op jit(solution)/shard_map/ppermute | solution.py:19
  70.8 3.9 %collective-permute-done.3 = f32[2,2,10,24,4]{4,3,2,1,0:T(8,128)S(1)} collective-permute-done((f32[2,2,10,24,4]{4,3,2,1,0:T(8,128)S(1)}, f32[2,2,10,24,4]{4,3,2,1,0:T(8,128)S(1)}, u32[]{:S(2)}, u32[]{:S(2)}) %collective-permute-start.3) | collective-permute-done | bytes 15392 | tf_op jit(solution)/shard_map/ppermute | solution.py:21
  74.7 0.6 pad_maximum_fusion
  75.3 1.3 fusion.95
  76.6 0.5 fusion.101
  77.1 5.0 %fusion.103 = (f32[2,10,20,132]{3,2,1,0:T(8,128)S(1)}, f32[2,10,20,132]{3,2,1,0:T(8,128)}, f32[2,10,20,132]{3,2,1,0:T(8,128)}, f32[2,10,20,132]{3,2,1,0:T(8,128)...) fusion(f32[2,1,10,22,134]{4,3,2,1,0:T(8,128)S(1)} %fusion.101), kind=kLoop, calls=%fused_computation.200 | loop fusion | flops 580800 | bytes 4995840 | tf_op jit(solution)/shard_map/mul | solution.py:66
  82.1 2.6 %fusion.133 = (f32[2,10,20,132]{3,2,1,0:T(8,128)}, f32[2,10,20,132]{3,2,1,0:T(8,128)}, f32[2,10,20,132]{3,2,1,0:T(8,128)}, f32[2,10,20,132]{3,2,1,0:T(8,128)}, f...) fusion(f32[2,1,10,22,134]{4,3,2,1,0:T(8,128)S(1)} %fusion.101), kind=kLoop, calls=%fused_computation.240 | loop fusion | flops 158400 | bytes 3379200 | tf_op jit(solution)/shard_map/mul | solution.py:66
  84.7 1.0 slice_bitcast_fusion.1
  85.7 0.8 slice_bitcast_fusion.8
  86.5 0.3 broadcast_multiply_fusion.1
  86.9 0.3 copy-done.2
  87.2 8.9 %broadcast_multiply_fusion.2 = (f32[2,2,10,20,132]{4,3,2,1,0:T(8,128)S(1)}, f32[2,2,10,20,132]{4,3,2,1,0:T(8,128)S(1)}, f32[2,2,10,20,132]{4,3,2,1,0:T(8,128)S(1)}) fusion(f32[2,10,20,132]{3,2,1,0:T(8,128)} %get-tuple-element.57, f32[2,10,20,132]{3,2,1,0:T(8,128)S(1)} %multiply_add_fusion.1, f32[2,2,10,22,134]{4,3,2,1,0:T(8,128)S(1)} %get-tuple-element.25, ...), kind=kLoop, calls=%fused_computation.252 | loop fusion | flops 10032000 | bytes 17623040 | tf_op jit(solution)/shard_map/mul | solution.py:110
  96.1 5.9 %broadcast_multiply_fusion = (f32[2,2,10,18,130]{4,3,2,1,0:T(8,128)S(1)}, f32[2,2,10,18,130]{4,3,2,1,0:T(8,128)S(1)}) fusion(f32[2,10,18,130]{3,2,1,0:T(8,128)} %slice_bitcast_fusion.1, f32[2,10,18,130]{3,2,1,0:T(8,128)S(1)} %slice_bitcast_fusion, f32[2,2,10,20,132]{4,3,2,1,0:T(8,128)S(1)} %get-tuple-element.22, f32[2]{0:T(128)S(1)} %copy-done.5, ...), kind=kLoop, calls=%fused_computation.249 | loop fusion | flops 5335200 | bytes 12243008 | tf_op jit(solution)/shard_map/mul | solution.py:110
  102.0 1.8 multiply_reduce_fusion.1
  103.8 51.0 %all-reduce.5 = (f32[2]{0:T(128)S(1)}, f32[2]{0:T(128)S(1)}, f32[2]{0:T(128)S(1)}, f32[2]{0:T(128)S(1)}) all-reduce(f32[2]{0:T(128)S(1)} %get-tuple-element.27, f32[2]{0:T(128)S(1)} %get-tuple-element.6, f32[2]{0:T(128)S(1)} %get-tuple-element.7, ...), channel_id=1, replica_groups=mesh['group'=2,'plane'=16,'planey'=8,'ens'=2] {'plane'}, use_global_device_ids=true, to_apply=%region_11.12 | all-reduce | flops 8 | bytes 64 | tf_op jit(solution)/shard_map/psum | solution.py:30
  154.8 13.3 %all-reduce.6 = (f32[2]{0:T(128)S(1)}, f32[2]{0:T(128)S(1)}, f32[2]{0:T(128)S(1)}, f32[2]{0:T(128)S(1)}) all-reduce(f32[2]{0:T(128)S(1)} %get-tuple-element.8, f32[2]{0:T(128)S(1)} %get-tuple-element.9, f32[2]{0:T(128)S(1)} %get-tuple-element.10, ...), channel_id=1, replica_groups=mesh['group'=2,'plane'=16,'planey'=8,'ens'=2] {'planey'}, use_global_device_ids=true, to_apply=%region_12.13 | all-reduce | flops 8 | bytes 64 | tf_op jit(solution)/shard_map/psum | solution.py:30
  168.2 0.3 fusion.184
  168.5 19.0 %all-gather = f32[4,10,16,128]{3,2,1,0:T(8,128)S(1)} all-gather(f32[2,10,16,128]{3,2,1,0:T(8,128)S(1)} %fusion.184), channel_id=2, replica_groups=mesh['group'=2,'plane'=16,'planey'=8,'ens'=2] {'ens'}, dimensions={0}, use_global_device_ids=true | all-gather | bytes 491520 | tf_op jit(solution)/shard_map/all_gather | solution.py:35
  187.5 0.7 broadcast_multiply_fusion.3
  (44 shorter events, 0.9 us)
Async XLA Ops:
  0.7 25.5 %collective-permute-start.4 = (f32[1,1,1,4,128]{4,3,2,1,0:T(4,128)S(1)}, f32[1,1,1,4,128]{4,3,2,1,0:T(4,128)S(1)}, u32[]{:S(2)}, u32[]{:S(2)}) collective-permute-start(f32[1,1,1,4,128]{4,3,2,1,0:T(4,128)S(1)} %get-tuple-element.76), channel_id=1, source_target_pairs={{0,16},{16,32},{32,48},{48,64},{64,80},{80,96},{96,112},{112,128},... | collective-permute-start | bytes 6152 | tf_op jit(solution)/shard_map/ppermute | solution.py:19
  7.3 20.3 %collective-permute-start.5 = (f32[1,1,1,4,128]{4,3,2,1,0:T(4,128)S(1)}, f32[1,1,1,4,128]{4,3,2,1,0:T(4,128)S(1)}, u32[]{:S(2)}, u32[]{:S(2)}) collective-permute-start(f32[1,1,1,4,128]{4,3,2,1,0:T(4,128)S(1)} %get-tuple-element.77), channel_id=1, source_target_pairs={{16,0},{32,16},{48,32},{64,48},{80,64},{96,80},{112,96},{128,112},... | collective-permute-start | bytes 6152 | tf_op jit(solution)/shard_map/ppermute | solution.py:21
  9.3 26.0 %collective-permute-start.8 = (f32[1,1,1,4,128]{4,3,2,1,0:T(4,128)S(1)}, f32[1,1,1,4,128]{4,3,2,1,0:T(4,128)S(1)}, u32[]{:S(2)}, u32[]{:S(2)}) collective-permute-start(f32[1,1,1,4,128]{4,3,2,1,0:T(4,128)S(1)} %get-tuple-element.74), channel_id=1, source_target_pairs={{0,16},{16,32},{32,48},{48,64},{64,80},{80,96},{96,112},{112,128},... | collective-permute-start | bytes 6152 | tf_op jit(solution)/shard_map/ppermute | solution.py:19
  15.7 22.9 %collective-permute-start.9 = (f32[1,1,1,4,128]{4,3,2,1,0:T(4,128)S(1)}, f32[1,1,1,4,128]{4,3,2,1,0:T(4,128)S(1)}, u32[]{:S(2)}, u32[]{:S(2)}) collective-permute-start(f32[1,1,1,4,128]{4,3,2,1,0:T(4,128)S(1)} %get-tuple-element.75), channel_id=1, source_target_pairs={{16,0},{32,16},{48,32},{64,48},{80,64},{96,80},{112,96},{128,112},... | collective-permute-start | bytes 6152 | tf_op jit(solution)/shard_map/ppermute | solution.py:21
  18.7 30.1 %collective-permute-start.12 = (f32[2,1,1,4,128]{4,3,0,2,1:T(4,128)S(1)}, f32[2,1,1,4,128]{4,3,0,2,1:T(4,128)S(1)}, u32[]{:S(2)}, u32[]{:S(2)}) collective-permute-start(f32[2,1,1,4,128]{4,3,0,2,1:T(4,128)S(1)} %get-tuple-element.68), channel_id=1, source_target_pairs={{0,16},{16,32},{32,48},{48,64},{64,80},{80,96},{96,112},{112,128},... | collective-permute-start | bytes 12296 | tf_op jit(solution)/shard_map/ppermute | solution.py:19
  26.2 22.6 %collective-permute-start.13 = (f32[2,1,1,4,128]{4,3,0,2,1:T(4,128)S(1)}, f32[2,1,1,4,128]{4,3,0,2,1:T(4,128)S(1)}, u32[]{:S(2)}, u32[]{:S(2)}) collective-permute-start(f32[2,1,1,4,128]{4,3,0,2,1:T(4,128)S(1)} %get-tuple-element.69), channel_id=1, source_target_pairs={{16,0},{32,16},{48,32},{64,48},{80,64},{96,80},{112,96},{128,112},... | collective-permute-start | bytes 12296 | tf_op jit(solution)/shard_map/ppermute | solution.py:21
  27.5 32.0 %collective-permute-start = (f32[2,2,10,4,128]{4,3,2,1,0:T(4,128)S(1)}, f32[2,2,10,4,128]{4,3,2,1,0:T(4,128)S(1)}, u32[]{:S(2)}, u32[]{:S(2)}) collective-permute-start(f32[2,2,10,4,128]{4,3,2,1,0:T(4,128)S(1)} %get-tuple-element.60), channel_id=1, source_target_pairs={{0,16},{16,32},{32,48},{48,64},{64,80},{80,96},{96,112},{112,128},... | collective-permute-start | bytes 245768 | tf_op jit(solution)/shard_map/ppermute | solution.py:19
  35.3 4.7 %collective-permute-start.6 = (f32[1,1,1,24,4]{4,3,2,1,0:T(8,128)S(1)}, f32[1,1,1,24,4]{4,3,2,1,0:T(8,128)S(1)}, u32[]{:S(2)}, u32[]{:S(2)}) collective-permute-start(f32[1,1,1,24,4]{4,3,2,1,0:T(8,128)S(1)} %get-tuple-element.72), channel_id=1, source_target_pairs={{0,2},{2,4},{4,6},{6,8},{8,10},{10,12},{12,14},{1,3},{3,5},{5,7},{... | collective-permute-start | bytes 1160 | tf_op jit(solution)/shard_map/ppermute | solution.py:19
  38.5 5.4 %collective-permute-start.7 = (f32[1,1,1,24,4]{4,3,2,1,0:T(8,128)S(1)}, f32[1,1,1,24,4]{4,3,2,1,0:T(8,128)S(1)}, u32[]{:S(2)}, u32[]{:S(2)}) collective-permute-start(f32[1,1,1,24,4]{4,3,2,1,0:T(8,128)S(1)} %get-tuple-element.73), channel_id=1, source_target_pairs={{2,0},{4,2},{6,4},{8,6},{10,8},{12,10},{14,12},{3,1},{5,3},{7,5},{... | collective-permute-start | bytes 1160 | tf_op jit(solution)/shard_map/ppermute | solution.py:21
  40.0 5.4 %collective-permute-start.10 = (f32[1,1,1,24,4]{4,3,2,1,0:T(8,128)S(1)}, f32[1,1,1,24,4]{4,3,2,1,0:T(8,128)S(1)}, u32[]{:S(2)}, u32[]{:S(2)}) collective-permute-start(f32[1,1,1,24,4]{4,3,2,1,0:T(8,128)S(1)} %get-tuple-element.70), channel_id=1, source_target_pairs={{0,2},{2,4},{4,6},{6,8},{8,10},{10,12},{12,14},{1,3},{3,5},{5,7},{... | collective-permute-start | bytes 1160 | tf_op jit(solution)/shard_map/ppermute | solution.py:19
  44.0 4.6 %collective-permute-start.11 = (f32[1,1,1,24,4]{4,3,2,1,0:T(8,128)S(1)}, f32[1,1,1,24,4]{4,3,2,1,0:T(8,128)S(1)}, u32[]{:S(2)}, u32[]{:S(2)}) collective-permute-start(f32[1,1,1,24,4]{4,3,2,1,0:T(8,128)S(1)} %get-tuple-element.71), channel_id=1, source_target_pairs={{2,0},{4,2},{6,4},{8,6},{10,8},{12,10},{14,12},{3,1},{5,3},{7,5},{... | collective-permute-start | bytes 1160 | tf_op jit(solution)/shard_map/ppermute | solution.py:21
  45.4 14.1 %collective-permute-start.1 = (f32[2,2,10,4,128]{4,3,2,1,0:T(4,128)S(1)}, f32[2,2,10,4,128]{4,3,2,1,0:T(4,128)S(1)}, u32[]{:S(2)}, u32[]{:S(2)}) collective-permute-start(f32[2,2,10,4,128]{4,3,2,1,0:T(4,128)S(1)} %get-tuple-element.61), channel_id=1, source_target_pairs={{16,0},{32,16},{48,32},{64,48},{80,64},{96,80},{112,96},{128,112},... | collective-permute-start | bytes 245768 | tf_op jit(solution)/shard_map/ppermute | solution.py:21
  48.9 5.5 %collective-permute-start.14 = (f32[2,1,1,24,4]{4,3,0,2,1:T(8,128)S(1)}, f32[2,1,1,24,4]{4,3,0,2,1:T(8,128)S(1)}, u32[]{:S(2)}, u32[]{:S(2)}) collective-permute-start(f32[2,1,1,24,4]{4,3,0,2,1:T(8,128)S(1)} %get-tuple-element.66), channel_id=1, source_target_pairs={{0,2},{2,4},{4,6},{6,8},{8,10},{10,12},{12,14},{1,3},{3,5},{5,7},{... | collective-permute-start | bytes 2312 | tf_op jit(solution)/shard_map/ppermute | solution.py:19
  53.1 5.8 %collective-permute-start.15 = (f32[2,1,1,24,4]{4,3,0,2,1:T(8,128)S(1)}, f32[2,1,1,24,4]{4,3,0,2,1:T(8,128)S(1)}, u32[]{:S(2)}, u32[]{:S(2)}) collective-permute-start(f32[2,1,1,24,4]{4,3,0,2,1:T(8,128)S(1)} %get-tuple-element.67), channel_id=1, source_target_pairs={{2,0},{4,2},{6,4},{8,6},{10,8},{12,10},{14,12},{3,1},{5,3},{7,5},{... | collective-permute-start | bytes 2312 | tf_op jit(solution)/shard_map/ppermute | solution.py:21
  59.1 1.0 copy-start
  60.3 10.5 %collective-permute-start.2 = (f32[2,2,10,24,4]{4,3,2,1,0:T(8,128)S(1)}, f32[2,2,10,24,4]{4,3,2,1,0:T(8,128)S(1)}, u32[]{:S(2)}, u32[]{:S(2)}) collective-permute-start(f32[2,2,10,24,4]{4,3,2,1,0:T(8,128)S(1)} %get-tuple-element.58), channel_id=1, source_target_pairs={{0,2},{2,4},{4,6},{6,8},{8,10},{10,12},{12,14},{1,3},{3,5},{5,7},{... | collective-permute-start | bytes 46088 | tf_op jit(solution)/shard_map/ppermute | solution.py:19
  64.9 9.7 %collective-permute-start.3 = (f32[2,2,10,24,4]{4,3,2,1,0:T(8,128)S(1)}, f32[2,2,10,24,4]{4,3,2,1,0:T(8,128)S(1)}, u32[]{:S(2)}, u32[]{:S(2)}) collective-permute-start(f32[2,2,10,24,4]{4,3,2,1,0:T(8,128)S(1)} %get-tuple-element.59), channel_id=1, source_target_pairs={{2,0},{4,2},{6,4},{8,6},{10,8},{12,10},{14,12},{3,1},{5,3},{7,5},{... | collective-permute-start | bytes 46088 | tf_op jit(solution)/shard_map/ppermute | solution.py:21
  86.5 0.7 copy-start.2
  86.5 0.7 copy-start.3
  86.5 0.7 copy-start.4
  86.5 0.7 copy-start.5
  96.1 5.9 %copy-start.1 = (f32[2,10,16,128]{3,2,1,0:T(8,128)S(1)}, f32[2,10,16,128]{3,2,1,0:T(8,128)}, u32[]{:S(2)}) copy-start(f32[2,10,16,128]{3,2,1,0:T(8,128)} %slice_bitcast_fusion.8) | copy-start | bytes 491524
where the time goes:
time: 189 us; the launch traced here: 188 us
  blocking collectives  83.3 us (44%)
  starting transfers between devices  53.7 us (28%)
  other arithmetic  31.8 us (17%)
  waiting for transfers between devices  14.5 us (8%)
  local copies, waits for them, and re-layouts  4.53 us (2%)
    psum x2, blocking collectives, one_axis_at_a_time(): value = lax.psum(value, axis)  64.3 us
    ppermute x8, starting transfers between devices, extended_2(): lax.ppermute(tail, axis, [(i, (i + 1) % count) for i in range(ends)])  43 us
    all_gather x1, blocking collectives, total_of_pieces(): blocks = lax.all_gather(value, axis)  19 us
    mul x3, other arithmetic, apply_local(): product = roots_wide * field_wide  15.1 us
    ppermute x8, starting transfers between devices, extended_2(): lax.ppermute(head, axis, [((i + 1) % count, i) for i in range(ends)])  10.6 us
    ppermute x8, waiting for transfers between devices, extended_2(): lax.ppermute(head, axis, [((i + 1) % count, i) for i in range(ends)])  10.2 us
    mul x2, other arithmetic, neighbour_sum(): addend = coefficient((step_z, step_x, step_y)) * window  7.57 us
    ppermute x8, waiting for transfers between devices, extended_2(): lax.ppermute(tail, axis, [(i, (i + 1) % count) for i in range(ends)])  4.27 us
  transfers between devices with their start and end apart: 16, of which 4 were waited for; matrix products, arithmetic and copies ran while one was open for 2% of the time, Pallas kernels for 0%

commit v1 on v0

--- a/solution.py
+++ b/solution.py
@@ -27,7 +27,7 @@
 
 def one_axis_at_a_time(value, axes):
     for axis in axes:
-        value = lax.psum(value, axis)
+        value = jnp.sum(lax.all_gather(value, axis), axis=0)
     return value
 
 

time: 189 us -> 196 us (1.037)
  local copies, waits for them, and re-layouts: 4.53 us -> 9.47 us
    psum x2 -> x0, blocking collectives: 64.3 us -> none  [one_axis_at_a_time(): value = lax.psum(value, axis)]
    unnamed x0 -> x2, blocking collectives: none -> 64.3 us
    unnamed x12 -> x30, local copies, waits for them, and re-layouts: 0.87 us -> 5.19 us
  transfers between devices with their start and end apart: 16 -> 16, of which waited for: 4 -> 4; matrix products, arithmetic and copies ran while one was open for 2% -> 4% of each run, Pallas kernels for 0% -> 0%
where the time goes in v1:
time: 196 us; the launch traced here: 195 us
  blocking collectives  83.3 us (42%)
  starting transfers between devices  53.6 us (27%)
  other arithmetic  32.1 us (16%)
  waiting for transfers between devices  14.6 us (7%)
  local copies, waits for them, and re-layouts  9.47 us (5%)
    unnamed x2, blocking collectives  64.3 us
    ppermute x8, starting transfers between devices, extended_2(): lax.ppermute(tail, axis, [(i, (i + 1) % count) for i in range(ends)])  43.1 us
    all_gather x1, blocking collectives, total_of_pieces(): blocks = lax.all_gather(value, axis)  19 us
    mul x3, other arithmetic, apply_local(): product = roots_wide * field_wide  15.3 us
    ppermute x8, starting transfers between devices, extended_2(): lax.ppermute(head, axis, [((i + 1) % count, i) for i in range(ends)])  10.5 us
    ppermute x8, waiting for transfers between devices, extended_2(): lax.ppermute(head, axis, [((i + 1) % count, i) for i in range(ends)])  10.1 us
    mul x2, other arithmetic, neighbour_sum(): addend = coefficient((step_z, step_x, step_y)) * window  7.57 us
    unnamed x30, local copies, waits for them, and re-layouts  5.19 us
  transfers between devices with their start and end apart: 16, of which 4 were waited for; matrix products, arithmetic and copies ran while one was open for 4% of the time, Pallas kernels for 0%

profile of v1, /device:TPU:65, one launch (start us, length us, event | category | flops | bytes accessed | tf_op | source)
XLA Modules:
  0.0 194.8 jit_solution(13563276036835238565)
XLA Ops:
  0.0 0.7 convert_bitcast_fusion
  0.7 6.6 %collective-permute-start.4 = (f32[1,1,1,4,128]{4,3,2,1,0:T(4,128)S(1)}, f32[1,1,1,4,128]{4,3,2,1,0:T(4,128)S(1)}, u32[]{:S(2)}, u32[]{:S(2)}) collective-permute-start(f32[1,1,1,4,128]{4,3,2,1,0:T(4,128)S(1)} %get-tuple-element.76), channel_id=1, source_target_pairs={{0,16},{16,32},{32,48},{48,64},{64,80},{80,96},{96,112},{112,128},... | collective-permute-start | bytes 6152 | tf_op jit(solution)/shard_map/ppermute | solution.py:19
  7.3 1.3 collective-permute-start.5
  8.6 0.7 multiply_bitcast_fusion
  9.3 6.4 %collective-permute-start.8 = (f32[1,1,1,4,128]{4,3,2,1,0:T(4,128)S(1)}, f32[1,1,1,4,128]{4,3,2,1,0:T(4,128)S(1)}, u32[]{:S(2)}, u32[]{:S(2)}) collective-permute-start(f32[1,1,1,4,128]{4,3,2,1,0:T(4,128)S(1)} %get-tuple-element.74), channel_id=1, source_target_pairs={{0,16},{16,32},{32,48},{48,64},{64,80},{80,96},{96,112},{112,128},... | collective-permute-start | bytes 6152 | tf_op jit(solution)/shard_map/ppermute | solution.py:19
  15.7 1.3 collective-permute-start.9
  17.0 0.7 compare_convert_fusion.1
  17.7 1.0 multiply_reduce_fusion.3
  18.7 6.4 %collective-permute-start.12 = (f32[2,1,1,4,128]{4,3,0,2,1:T(4,128)S(1)}, f32[2,1,1,4,128]{4,3,0,2,1:T(4,128)S(1)}, u32[]{:S(2)}, u32[]{:S(2)}) collective-permute-start(f32[2,1,1,4,128]{4,3,0,2,1:T(4,128)S(1)} %get-tuple-element.68), channel_id=1, source_target_pairs={{0,16},{16,32},{32,48},{48,64},{64,80},{80,96},{96,112},{112,128},... | collective-permute-start | bytes 12296 | tf_op jit(solution)/shard_map/ppermute | solution.py:19
  25.2 1.0 fusion.197
  26.2 1.3 dynamic-slice
  27.5 1.3 dynamic-slice.1
  30.0 1.3 collective-permute-start.13
  31.4 7.6 %collective-permute-start = (f32[2,2,10,4,128]{4,3,2,1,0:T(4,128)S(1)}, f32[2,2,10,4,128]{4,3,2,1,0:T(4,128)S(1)}, u32[]{:S(2)}, u32[]{:S(2)}) collective-permute-start(f32[2,2,10,4,128]{4,3,2,1,0:T(4,128)S(1)} %get-tuple-element.60), channel_id=1, source_target_pairs={{0,16},{16,32},{32,48},{48,64},{64,80},{80,96},{96,112},{112,128},... | collective-permute-start | bytes 245768 | tf_op jit(solution)/shard_map/ppermute | solution.py:19
  39.1 3.3 %collective-permute-start.6 = (f32[1,1,1,24,4]{4,3,2,1,0:T(8,128)S(1)}, f32[1,1,1,24,4]{4,3,2,1,0:T(8,128)S(1)}, u32[]{:S(2)}, u32[]{:S(2)}) collective-permute-start(f32[1,1,1,24,4]{4,3,2,1,0:T(8,128)S(1)} %get-tuple-element.72), channel_id=1, source_target_pairs={{0,2},{2,4},{4,6},{6,8},{8,10},{10,12},{12,14},{1,3},{3,5},{5,7},{... | collective-permute-start | bytes 1160 | tf_op jit(solution)/shard_map/ppermute | solution.py:19
  42.4 1.3 collective-permute-start.7
  43.8 4.0 %collective-permute-start.10 = (f32[1,1,1,24,4]{4,3,2,1,0:T(8,128)S(1)}, f32[1,1,1,24,4]{4,3,2,1,0:T(8,128)S(1)}, u32[]{:S(2)}, u32[]{:S(2)}) collective-permute-start(f32[1,1,1,24,4]{4,3,2,1,0:T(8,128)S(1)} %get-tuple-element.70), channel_id=1, source_target_pairs={{0,2},{2,4},{4,6},{6,8},{8,10},{10,12},{12,14},{1,3},{3,5},{5,7},{... | collective-permute-start | bytes 1160 | tf_op jit(solution)/shard_map/ppermute | solution.py:19
  47.8 1.3 collective-permute-start.11
  49.2 1.3 collective-permute-start.1
  50.5 1.7 collective-permute-done.11
  52.7 4.3 %collective-permute-start.14 = (f32[2,1,1,24,4]{4,3,0,2,1:T(8,128)S(1)}, f32[2,1,1,24,4]{4,3,0,2,1:T(8,128)S(1)}, u32[]{:S(2)}, u32[]{:S(2)}) collective-permute-start(f32[2,1,1,24,4]{4,3,0,2,1:T(8,128)S(1)} %get-tuple-element.66), channel_id=1, source_target_pairs={{0,2},{2,4},{4,6},{6,8},{8,10},{10,12},{12,14},{1,3},{3,5},{5,7},{... | collective-permute-start | bytes 2312 | tf_op jit(solution)/shard_map/ppermute | solution.py:19
  56.9 1.3 collective-permute-start.15
  58.3 4.5 %collective-permute-done.15 = f32[2,1,1,24,4]{4,3,0,2,1:T(8,128)S(1)} collective-permute-done((f32[2,1,1,24,4]{4,3,0,2,1:T(8,128)S(1)}, f32[2,1,1,24,4]{4,3,0,2,1:T(8,128)S(1)}, u32[]{:S(2)}, u32[]{:S(2)}) %collective-permute-start.15) | collective-permute-done | bytes 800 | tf_op jit(solution)/shard_map/ppermute | solution.py:21
  63.3 0.5 copy-done
  64.1 4.6 %collective-permute-start.2 = (f32[2,2,10,24,4]{4,3,2,1,0:T(8,128)S(1)}, f32[2,2,10,24,4]{4,3,2,1,0:T(8,128)S(1)}, u32[]{:S(2)}, u32[]{:S(2)}) collective-permute-start(f32[2,2,10,24,4]{4,3,2,1,0:T(8,128)S(1)} %get-tuple-element.58), channel_id=1, source_target_pairs={{0,2},{2,4},{4,6},{6,8},{8,10},{10,12},{12,14},{1,3},{3,5},{5,7},{... | collective-permute-start | bytes 46088 | tf_op jit(solution)/shard_map/ppermute | solution.py:19
  68.8 1.3 collective-permute-start.3
  70.2 4.4 %collective-permute-done.2 = f32[2,2,10,24,4]{4,3,2,1,0:T(8,128)S(1)} collective-permute-done((f32[2,2,10,24,4]{4,3,2,1,0:T(8,128)S(1)}, f32[2,2,10,24,4]{4,3,2,1,0:T(8,128)S(1)}, u32[]{:S(2)}, u32[]{:S(2)}) %collective-permute-start.2) | collective-permute-done | bytes 15392 | tf_op jit(solution)/shard_map/ppermute | solution.py:19
  74.6 3.9 %collective-permute-done.3 = f32[2,2,10,24,4]{4,3,2,1,0:T(8,128)S(1)} collective-permute-done((f32[2,2,10,24,4]{4,3,2,1,0:T(8,128)S(1)}, f32[2,2,10,24,4]{4,3,2,1,0:T(8,128)S(1)}, u32[]{:S(2)}, u32[]{:S(2)}) %collective-permute-start.3) | collective-permute-done | bytes 15392 | tf_op jit(solution)/shard_map/ppermute | solution.py:21
  78.5 0.6 pad_maximum_fusion
  79.1 1.3 fusion.95
  80.4 0.5 fusion.101
  80.9 5.0 %fusion.103 = (f32[2,10,20,132]{3,2,1,0:T(8,128)S(1)}, f32[2,10,20,132]{3,2,1,0:T(8,128)}, f32[2,10,20,132]{3,2,1,0:T(8,128)}, f32[2,10,20,132]{3,2,1,0:T(8,128)...) fusion(f32[2,1,10,22,134]{4,3,2,1,0:T(8,128)S(1)} %fusion.101), kind=kLoop, calls=%fused_computation.200 | loop fusion | flops 580800 | bytes 4995840 | tf_op jit(solution)/shard_map/mul | solution.py:66
  85.9 2.6 %fusion.133 = (f32[2,10,20,132]{3,2,1,0:T(8,128)}, f32[2,10,20,132]{3,2,1,0:T(8,128)}, f32[2,10,20,132]{3,2,1,0:T(8,128)}, f32[2,10,20,132]{3,2,1,0:T(8,128)}, f...) fusion(f32[2,1,10,22,134]{4,3,2,1,0:T(8,128)S(1)} %fusion.101), kind=kLoop, calls=%fused_computation.240 | loop fusion | flops 158400 | bytes 3379200 | tf_op jit(solution)/shard_map/mul | solution.py:66
  88.5 1.0 slice_bitcast_fusion.1
  89.5 0.8 slice_bitcast_fusion.8
  90.3 0.3 broadcast_multiply_fusion.1
  90.6 0.3 copy-done.2
  91.0 9.1 %broadcast_multiply_fusion.2 = (f32[2,2,10,20,132]{4,3,2,1,0:T(8,128)S(1)}, f32[2,2,10,20,132]{4,3,2,1,0:T(8,128)S(1)}, f32[2,2,10,20,132]{4,3,2,1,0:T(8,128)S(1)}) fusion(f32[2,10,20,132]{3,2,1,0:T(8,128)} %get-tuple-element.57, f32[2,10,20,132]{3,2,1,0:T(8,128)S(1)} %multiply_add_fusion.1, f32[2,2,10,22,134]{4,3,2,1,0:T(8,128)S(1)} %get-tuple-element.25, ...), kind=kLoop, calls=%fused_computation.252 | loop fusion | flops 10032000 | bytes 17623040 | tf_op jit(solution)/shard_map/mul | solution.py:110
  100.1 5.9 %broadcast_multiply_fusion = (f32[2,2,10,18,130]{4,3,2,1,0:T(8,128)S(1)}, f32[2,2,10,18,130]{4,3,2,1,0:T(8,128)S(1)}) fusion(f32[2,10,18,130]{3,2,1,0:T(8,128)} %slice_bitcast_fusion.1, f32[2,10,18,130]{3,2,1,0:T(8,128)S(1)} %slice_bitcast_fusion, f32[2,2,10,20,132]{4,3,2,1,0:T(8,128)S(1)} %get-tuple-element.22, f32[2]{0:T(128)S(1)} %copy-done.5, ...), kind=kLoop, calls=%fused_computation.249 | loop fusion | flops 5335200 | bytes 12243008 | tf_op jit(solution)/shard_map/mul | solution.py:110
  106.0 1.8 multiply_reduce_fusion.1
  108.6 50.9 %all-reduce.13 = (f32[32]{0:T(128)S(1)}, f32[32]{0:T(128)S(1)}, f32[32]{0:T(128)S(1)}, f32[32]{0:T(128)S(1)}) all-reduce(f32[32]{0:T(128)S(1)} %dynamic-update-slice.6, f32[32]{0:T(128)S(1)} %dynamic-update-slice.4, f32[32]{0:T(128)S(1)} %dynamic-update-slice, ...), channel_id=8, replica_groups=mesh['group'=2,'plane'=16,'planey'=8,'ens'=2] {'plane'}, use_global_device_ids=true, to_apply=%add.11 | all-reduce | flops 128 | bytes 1024
  160.0 0.2 dynamic-update-slice.1
  160.5 0.2 dynamic-update-slice.5
  160.7 0.2 dynamic-update-slice.7
  161.0 13.4 %all-reduce.14 = (f32[16]{0:T(128)S(1)}, f32[16]{0:T(128)S(1)}, f32[16]{0:T(128)S(1)}, f32[16]{0:T(128)S(1)}) all-reduce(f32[16]{0:T(128)S(1)} %dynamic-update-slice.7, f32[16]{0:T(128)S(1)} %dynamic-update-slice.5, f32[16]{0:T(128)S(1)} %dynamic-update-slice.1, ...), channel_id=9, replica_groups=mesh['group'=2,'plane'=16,'planey'=8,'ens'=2] {'planey'}, use_global_device_ids=true, to_apply=%add.12 | all-reduce | flops 64 | bytes 512
  174.8 0.3 fusion.184
  175.1 19.0 %all-gather.8 = f32[4,10,16,128]{3,2,1,0:T(8,128)S(1)} all-gather(f32[2,10,16,128]{3,2,1,0:T(8,128)S(1)} %fusion.184), channel_id=10, replica_groups=mesh['group'=2,'plane'=16,'planey'=8,'ens'=2] {'ens'}, dimensions={0}, use_global_device_ids=true | all-gather | bytes 491520 | tf_op jit(solution)/shard_map/all_gather | solution.py:35
  194.1 0.7 broadcast_multiply_fusion.3
  (78 shorter events, 3.6 us)
Async XLA Ops:
  0.7 29.3 %collective-permute-start.4 = (f32[1,1,1,4,128]{4,3,2,1,0:T(4,128)S(1)}, f32[1,1,1,4,128]{4,3,2,1,0:T(4,128)S(1)}, u32[]{:S(2)}, u32[]{:S(2)}) collective-permute-start(f32[1,1,1,4,128]{4,3,2,1,0:T(4,128)S(1)} %get-tuple-element.76), channel_id=1, source_target_pairs={{0,16},{16,32},{32,48},{48,64},{64,80},{80,96},{96,112},{112,128},... | collective-permute-start | bytes 6152 | tf_op jit(solution)/shard_map/ppermute | solution.py:19
  7.3 24.1 %collective-permute-start.5 = (f32[1,1,1,4,128]{4,3,2,1,0:T(4,128)S(1)}, f32[1,1,1,4,128]{4,3,2,1,0:T(4,128)S(1)}, u32[]{:S(2)}, u32[]{:S(2)}) collective-permute-start(f32[1,1,1,4,128]{4,3,2,1,0:T(4,128)S(1)} %get-tuple-element.77), channel_id=1, source_target_pairs={{16,0},{32,16},{48,32},{64,48},{80,64},{96,80},{112,96},{128,112},... | collective-permute-start | bytes 6152 | tf_op jit(solution)/shard_map/ppermute | solution.py:21
  9.3 29.8 %collective-permute-start.8 = (f32[1,1,1,4,128]{4,3,2,1,0:T(4,128)S(1)}, f32[1,1,1,4,128]{4,3,2,1,0:T(4,128)S(1)}, u32[]{:S(2)}, u32[]{:S(2)}) collective-permute-start(f32[1,1,1,4,128]{4,3,2,1,0:T(4,128)S(1)} %get-tuple-element.74), channel_id=1, source_target_pairs={{0,16},{16,32},{32,48},{48,64},{64,80},{80,96},{96,112},{112,128},... | collective-permute-start | bytes 6152 | tf_op jit(solution)/shard_map/ppermute | solution.py:19
  15.7 26.7 %collective-permute-start.9 = (f32[1,1,1,4,128]{4,3,2,1,0:T(4,128)S(1)}, f32[1,1,1,4,128]{4,3,2,1,0:T(4,128)S(1)}, u32[]{:S(2)}, u32[]{:S(2)}) collective-permute-start(f32[1,1,1,4,128]{4,3,2,1,0:T(4,128)S(1)} %get-tuple-element.75), channel_id=1, source_target_pairs={{16,0},{32,16},{48,32},{64,48},{80,64},{96,80},{112,96},{128,112},... | collective-permute-start | bytes 6152 | tf_op jit(solution)/shard_map/ppermute | solution.py:21
  18.7 33.8 %collective-permute-start.12 = (f32[2,1,1,4,128]{4,3,0,2,1:T(4,128)S(1)}, f32[2,1,1,4,128]{4,3,0,2,1:T(4,128)S(1)}, u32[]{:S(2)}, u32[]{:S(2)}) collective-permute-start(f32[2,1,1,4,128]{4,3,0,2,1:T(4,128)S(1)} %get-tuple-element.68), channel_id=1, source_target_pairs={{0,16},{16,32},{32,48},{48,64},{64,80},{80,96},{96,112},{112,128},... | collective-permute-start | bytes 12296 | tf_op jit(solution)/shard_map/ppermute | solution.py:19
  30.0 22.5 %collective-permute-start.13 = (f32[2,1,1,4,128]{4,3,0,2,1:T(4,128)S(1)}, f32[2,1,1,4,128]{4,3,0,2,1:T(4,128)S(1)}, u32[]{:S(2)}, u32[]{:S(2)}) collective-permute-start(f32[2,1,1,4,128]{4,3,0,2,1:T(4,128)S(1)} %get-tuple-element.69), channel_id=1, source_target_pairs={{16,0},{32,16},{48,32},{64,48},{80,64},{96,80},{112,96},{128,112},... | collective-permute-start | bytes 12296 | tf_op jit(solution)/shard_map/ppermute | solution.py:21
  31.4 32.0 %collective-permute-start = (f32[2,2,10,4,128]{4,3,2,1,0:T(4,128)S(1)}, f32[2,2,10,4,128]{4,3,2,1,0:T(4,128)S(1)}, u32[]{:S(2)}, u32[]{:S(2)}) collective-permute-start(f32[2,2,10,4,128]{4,3,2,1,0:T(4,128)S(1)} %get-tuple-element.60), channel_id=1, source_target_pairs={{0,16},{16,32},{32,48},{48,64},{64,80},{80,96},{96,112},{112,128},... | collective-permute-start | bytes 245768 | tf_op jit(solution)/shard_map/ppermute | solution.py:19
  39.1 4.7 %collective-permute-start.6 = (f32[1,1,1,24,4]{4,3,2,1,0:T(8,128)S(1)}, f32[1,1,1,24,4]{4,3,2,1,0:T(8,128)S(1)}, u32[]{:S(2)}, u32[]{:S(2)}) collective-permute-start(f32[1,1,1,24,4]{4,3,2,1,0:T(8,128)S(1)} %get-tuple-element.72), channel_id=1, source_target_pairs={{0,2},{2,4},{4,6},{6,8},{8,10},{10,12},{12,14},{1,3},{3,5},{5,7},{... | collective-permute-start | bytes 1160 | tf_op jit(solution)/shard_map/ppermute | solution.py:19
  42.4 5.4 %collective-permute-start.7 = (f32[1,1,1,24,4]{4,3,2,1,0:T(8,128)S(1)}, f32[1,1,1,24,4]{4,3,2,1,0:T(8,128)S(1)}, u32[]{:S(2)}, u32[]{:S(2)}) collective-permute-start(f32[1,1,1,24,4]{4,3,2,1,0:T(8,128)S(1)} %get-tuple-element.73), channel_id=1, source_target_pairs={{2,0},{4,2},{6,4},{8,6},{10,8},{12,10},{14,12},{3,1},{5,3},{7,5},{... | collective-permute-start | bytes 1160 | tf_op jit(solution)/shard_map/ppermute | solution.py:21
  43.8 5.4 %collective-permute-start.10 = (f32[1,1,1,24,4]{4,3,2,1,0:T(8,128)S(1)}, f32[1,1,1,24,4]{4,3,2,1,0:T(8,128)S(1)}, u32[]{:S(2)}, u32[]{:S(2)}) collective-permute-start(f32[1,1,1,24,4]{4,3,2,1,0:T(8,128)S(1)} %get-tuple-element.70), channel_id=1, source_target_pairs={{0,2},{2,4},{4,6},{6,8},{8,10},{10,12},{12,14},{1,3},{3,5},{5,7},{... | collective-permute-start | bytes 1160 | tf_op jit(solution)/shard_map/ppermute | solution.py:19
  47.8 4.5 %collective-permute-start.11 = (f32[1,1,1,24,4]{4,3,2,1,0:T(8,128)S(1)}, f32[1,1,1,24,4]{4,3,2,1,0:T(8,128)S(1)}, u32[]{:S(2)}, u32[]{:S(2)}) collective-permute-start(f32[1,1,1,24,4]{4,3,2,1,0:T(8,128)S(1)} %get-tuple-element.71), channel_id=1, source_target_pairs={{2,0},{4,2},{6,4},{8,6},{10,8},{12,10},{14,12},{3,1},{5,3},{7,5},{... | collective-permute-start | bytes 1160 | tf_op jit(solution)/shard_map/ppermute | solution.py:21
  49.2 14.1 %collective-permute-start.1 = (f32[2,2,10,4,128]{4,3,2,1,0:T(4,128)S(1)}, f32[2,2,10,4,128]{4,3,2,1,0:T(4,128)S(1)}, u32[]{:S(2)}, u32[]{:S(2)}) collective-permute-start(f32[2,2,10,4,128]{4,3,2,1,0:T(4,128)S(1)} %get-tuple-element.61), channel_id=1, source_target_pairs={{16,0},{32,16},{48,32},{64,48},{80,64},{96,80},{112,96},{128,112},... | collective-permute-start | bytes 245768 | tf_op jit(solution)/shard_map/ppermute | solution.py:21
  52.7 5.6 %collective-permute-start.14 = (f32[2,1,1,24,4]{4,3,0,2,1:T(8,128)S(1)}, f32[2,1,1,24,4]{4,3,0,2,1:T(8,128)S(1)}, u32[]{:S(2)}, u32[]{:S(2)}) collective-permute-start(f32[2,1,1,24,4]{4,3,0,2,1:T(8,128)S(1)} %get-tuple-element.66), channel_id=1, source_target_pairs={{0,2},{2,4},{4,6},{6,8},{8,10},{10,12},{12,14},{1,3},{3,5},{5,7},{... | collective-permute-start | bytes 2312 | tf_op jit(solution)/shard_map/ppermute | solution.py:19
  56.9 5.8 %collective-permute-start.15 = (f32[2,1,1,24,4]{4,3,0,2,1:T(8,128)S(1)}, f32[2,1,1,24,4]{4,3,0,2,1:T(8,128)S(1)}, u32[]{:S(2)}, u32[]{:S(2)}) collective-permute-start(f32[2,1,1,24,4]{4,3,0,2,1:T(8,128)S(1)} %get-tuple-element.67), channel_id=1, source_target_pairs={{2,0},{4,2},{6,4},{8,6},{10,8},{12,10},{14,12},{3,1},{5,3},{7,5},{... | collective-permute-start | bytes 2312 | tf_op jit(solution)/shard_map/ppermute | solution.py:21
  62.9 1.0 copy-start
  64.1 10.5 %collective-permute-start.2 = (f32[2,2,10,24,4]{4,3,2,1,0:T(8,128)S(1)}, f32[2,2,10,24,4]{4,3,2,1,0:T(8,128)S(1)}, u32[]{:S(2)}, u32[]{:S(2)}) collective-permute-start(f32[2,2,10,24,4]{4,3,2,1,0:T(8,128)S(1)} %get-tuple-element.58), channel_id=1, source_target_pairs={{0,2},{2,4},{4,6},{6,8},{8,10},{10,12},{12,14},{1,3},{3,5},{5,7},{... | collective-permute-start | bytes 46088 | tf_op jit(solution)/shard_map/ppermute | solution.py:19
  68.8 9.7 %collective-permute-start.3 = (f32[2,2,10,24,4]{4,3,2,1,0:T(8,128)S(1)}, f32[2,2,10,24,4]{4,3,2,1,0:T(8,128)S(1)}, u32[]{:S(2)}, u32[]{:S(2)}) collective-permute-start(f32[2,2,10,24,4]{4,3,2,1,0:T(8,128)S(1)} %get-tuple-element.59), channel_id=1, source_target_pairs={{2,0},{4,2},{6,4},{8,6},{10,8},{12,10},{14,12},{3,1},{5,3},{7,5},{... | collective-permute-start | bytes 46088 | tf_op jit(solution)/shard_map/ppermute | solution.py:21
  90.3 0.7 copy-start.2
  90.3 0.7 copy-start.3
  90.3 0.7 copy-start.4
  90.3 0.7 copy-start.5
  100.1 5.9 %copy-start.1 = (f32[2,10,16,128]{3,2,1,0:T(8,128)S(1)}, f32[2,10,16,128]{3,2,1,0:T(8,128)}, u32[]{:S(2)}) copy-start(f32[2,10,16,128]{3,2,1,0:T(8,128)} %slice_bitcast_fusion.8) | copy-start | bytes 491524
